TPU v7x, 32 devices: a whole 2x2x4 slice. The times are simulated.
32 devices in a mesh: prow: 4 (over z), pcol: 8 (over y, x, core).
Axes of the slice: x: 2, y: 2, z: 4, core: 2. Of those that a mesh axis runs over, the one named last changes fastest.
Arguments:
- points: float32 [1, 8, 2, 1024], P(None, 'pcol'), may hold values from 0 to 1
- range_length: float32 [1], replicated, may hold values from 0.05 to 0.15
- smoothness: int32 [1], replicated, may hold values from 0 to 2
- sketch_bank: bfloat16 [8, 48, 1024], P('pcol'), may hold values from -6 to 6
- sketch_ids: int32 [2, 4, 1, 8], P(None, 'prow', None, 'pcol'), may hold values from 0 to 7
- tile_ranks: int32 [2, 4, 1, 8], P(None, 'prow', None, 'pcol'), may hold values from 16 to 48
Outputs:
- y_factors: float32 [2, 4, 1, 8, 48, 1024], P(None, 'prow', None, 'pcol')
- c_factors: float32 [2, 4, 1, 8, 48, 1024], P(None, 'prow', None, 'pcol')
- tile_error: float32 [2, 4, 1, 8], P(None, 'prow', None, 'pcol')
- rank_total: int32 [1], replicated
All inputs are finite; a program needn't handle non-finite values.
Results may differ from a plain program's by a relative error of at most 0.0098.
The roundings to bfloat16 on the way count: a program that leaves them out, or rounds other values in their place, can miss the bound.
Values may be sent and summed in bfloat16 or wider, within the bound.
A program may use at most 64 MiB of HBM per device.

v0:
```python
import jax
import jax.numpy as jnp
from jax import lax
from jax.sharding import PartitionSpec as P


def kernel_factors(smoothness, range_length):
    morton_value = smoothness[0].astype(jnp.float32)
    kernel_scale = jnp.sqrt(2.0 * morton_value + 1.0) / range_length[0]
    linear_factor = jnp.where(smoothness[0] >= 1, 1.0, 0.0).astype(jnp.float32)
    squared_distance = jnp.where(smoothness[0] >= 2, 1.0 / 3.0, 0.0).astype(jnp.float32)
    return (kernel_scale, linear_factor, squared_distance)


def covariance_tile(row_locations, column_locations, kernel_scale, linear_factor, squared_distance):
    offset_horizontal = row_locations[0][:, None] - column_locations[0][None, :]
    offset_vertical = row_locations[1][:, None] - column_locations[1][None, :]
    scaled_distance = kernel_scale * jnp.sqrt(
        offset_horizontal * offset_horizontal + offset_vertical * offset_vertical
    )
    return (
        1.0 + linear_factor * scaled_distance + squared_distance * scaled_distance * scaled_distance
    ) * jnp.exp(-scaled_distance)


def compress(tile_low, sketch, rank):
    keep = jnp.arange(sketch.shape[0]) < rank
    sketch = jnp.where(keep[:, None], sketch, jnp.zeros_like(sketch))
    sketched = lax.dot_general(
        sketch, tile_low, (((1,), (1,)), ((), ())), preferred_element_type=jnp.float32
    )
    product = jnp.dot(sketched.astype(jnp.bfloat16), tile_low, preferred_element_type=jnp.float32)
    gram = jnp.dot(sketched, sketched.T, precision=lax.Precision.HIGHEST)
    shift = 0.1 * jnp.trace(gram) / rank.astype(jnp.float32)
    gram = gram + jnp.diag(jnp.where(keep, shift, jnp.ones_like(shift)))
    factor = jnp.linalg.cholesky(gram)
    coeffs = jax.scipy.linalg.cho_solve((factor, True), product)
    approx = lax.dot_general(
        sketched, coeffs, (((0,), (0,)), ((), ())), precision=lax.Precision.HIGHEST
    )
    error = tile_low.astype(jnp.float32) - approx
    return (sketched, coeffs, jnp.sum(error * error))


def per_device(points, range_length, smoothness, sketch_bank, sketch_ids, tile_ranks):
    row_count = lax.axis_size("prow")
    col_count = lax.axis_size("pcol")
    row_place = lax.axis_index("prow")
    col_place = lax.axis_index("pcol")
    row_tiles = sketch_ids.shape[0]
    col_tiles = sketch_ids.shape[2]
    tile_size = points.shape[3]
    sketch_rows = sketch_bank.shape[1]
    slots_total = row_tiles * col_tiles
    tiles_across = col_tiles * col_count
    kernel_scale, linear_factor, squared_distance = kernel_factors(smoothness, range_length)
    gathered = lax.all_gather(points, "pcol", axis=1, tiled=True)
    every_block = gathered.reshape(tiles_across, 2, tile_size)
    row_index = jnp.arange(row_tiles, dtype=jnp.int32) * row_count + row_place
    col_index = jnp.arange(col_tiles, dtype=jnp.int32) * col_count + col_place
    slot_row = jnp.repeat(row_index, col_tiles)
    slot_col = jnp.tile(col_index, row_tiles)
    own_ids = sketch_ids.reshape(slots_total)
    own_ranks = tile_ranks.reshape(slots_total)
    lower = slot_col <= slot_row
    offdiag = slot_col < slot_row
    ranks_local = jnp.sum(jnp.where(offdiag, own_ranks, 0))
    rank_sum = lax.psum(ranks_local, ("prow", "pcol"))
    bank_whole = lax.all_gather(sketch_bank, "pcol", axis=0, tiled=True)
    chosen = bank_whole[own_ids]
    row_points_all = every_block[slot_row]
    col_points_all = every_block[slot_col]

    def one_tile(row_locations, column_locations, sketch, rank):
        tile_block = covariance_tile(
            row_locations, column_locations, kernel_scale, linear_factor, squared_distance
        )
        norm_sq = jnp.sum(tile_block * tile_block)
        sketched, coeffs, err_sq = compress(tile_block.astype(jnp.bfloat16), sketch, rank)
        return (sketched, coeffs, norm_sq, err_sq)

    def mapped(inputs):
        return one_tile(inputs[0], inputs[1], inputs[2], inputs[3])

    sketched_all, coeffs_all, norm_all, err_all = lax.map(
        mapped, (row_points_all, col_points_all, chosen, own_ranks)
    )
    norm_local = jnp.sum(jnp.where(lower, jnp.where(offdiag, 2.0, 1.0) * norm_all, 0.0))
    total = lax.psum(norm_local, ("prow", "pcol"))
    errors = (
        jnp.where(offdiag, jnp.sqrt(err_all), jnp.sqrt(norm_all)) * tiles_across / jnp.sqrt(total)
    )
    errors = jnp.where(lower, errors, 0.0)
    out_shape = (row_tiles, 1, col_tiles, 1, sketch_rows, tile_size)
    y_out = jnp.where(offdiag[:, None, None], sketched_all, 0.0).reshape(out_shape)
    c_out = jnp.where(offdiag[:, None, None], coeffs_all, 0.0).reshape(out_shape)
    err_out = errors.reshape(row_tiles, 1, col_tiles, 1)
    rank_out = rank_sum.reshape(1)
    return (y_out, c_out, err_out, rank_out)


def solution(mesh):
    in_specs = (
        P(None, "pcol", None, None),
        P(),
        P(),
        P("pcol", None, None),
        P(None, "prow", None, "pcol"),
        P(None, "prow", None, "pcol"),
    )
    out_specs = (
        P(None, "prow", None, "pcol", None, None),
        P(None, "prow", None, "pcol", None, None),
        P(None, "prow", None, "pcol"),
        P(),
    )
    return jax.shard_map(
        per_device, mesh=mesh, in_specs=in_specs, out_specs=out_specs, check_vma=False
    )
```

profile of v0, /device:TPU:0, one launch (start us, length us, event | category | flops | bytes accessed | tf_op | source)
XLA Modules:
  0.0 177.8 jit_solution(8479940237843029648)
XLA Ops:
  0.7 10.9 %all_gather.7 = f32[1,8,2,1024]{3,2,0,1:T(2,128)S(1)} all-gather(f32[1,1,2,1024]{3,2,0,1:T(2,128)} %bitcast.135), channel_id=1, replica_groups=mesh['prow'=4,'pcol'=8] {'pcol'}, dimensions={1}, use_global_device_ids=true | all-gather | bytes 73728 | tf_op jit(solution)/shard_map/all_gather | solution.py:57
  11.6 0.6 gather_fusion.2
  12.2 0.6 gather_fusion.1
  14.1 10.2 %all_gather.6 = bf16[8,48,1024]{2,1,0:T(8,128)(2,1)S(1)} all-gather(bf16[1,48,1024]{2,1,0:T(8,128)(2,1)} %param.11), channel_id=1, replica_groups=mesh['prow'=4,'pcol'=8] {'pcol'}, dimensions={0}, use_global_device_ids=true | all-gather | bytes 884736 | tf_op jit(solution)/shard_map/all_gather | solution.py:69
  24.4 0.6 gather_fusion
  25.0 68.5 %while.17 = (s32[]{:T(128)}, f32[2,48,1024]{2,1,0:T(8,128)S(1)}, f32[2,48,1024]{2,1,0:T(8,128)S(1)}, f32[2]{0:T(128)S(1)}, f32[2]{0:T(128)S(1)}, /*index=5*/s32[...) while((s32[]{:T(128)}, f32[2,48,1024]{2,1,0:T(8,128)S(1)}, ...), condition=%wide.region_6.7_spmd.clone, body=%wide.region_0.6_spmd.sunk.clone | while | flops 954344128 | bytes 2676799 | solution.py:85
  25.1 0.7 dynamic_slice.26
  25.8 0.7 iota_compare_fusion.6
  26.5 3.2 %bitcast_dynamic-update-slice_fusion.6 = (f32[2,48,1024]{2,1,0:T(8,128)S(1)}, f32[48,1024]{1,0:T(8,128)S(1)}) fusion(f32[2,48,1024]{2,1,0:T(8,128)S(1)} %get-tuple-element.256, s32[]{:T(128)} %get-tuple-element.255, f32[]{:T(128)} %get-tuple-element.278, f32[1024]{0:T(1024)S(1)} %bitcast.123, f32[1024]{0:T(1024)S(1)} %bitcast.127, ...), kind=kOutput, calls=%fused_computation.12.clone.1.clone | convolution fusion | flops 115392512 | bytes 510976 | tf_op jit(solution)/shard_map/while/body/eval_jaxpr/dot_general | solution.py:29
  29.6 0.9 select_reduce_fusion.7
  30.5 0.1 copy.15
  31.9 0.7 broadcast_select_fusion.3
  32.6 0.1 fusion.68
  32.7 4.4 %cholesky.73 = f32[48,48]{1,0:T(8,128)S(1)} custom-call(f32[48,48]{1,0:T(8,128)S(1)} %fusion.68), custom_call_target="Cholesky" | custom-call | tf_op jit(solution)/shard_map/while/body/eval_jaxpr/jit(cholesky)/cholesky | solution.py:36
  37.1 0.7 compare_reduce_fusion.3
  37.8 0.7 fusion.69
  38.5 3.7 %custom-call.20 = f32[1,48,48]{1,2,0:T(8,128)S(1)} custom-call(f32[1,48,48]{2,1,0:T(8,128)S(1)} %fusion.69), custom_call_target="InvertDiagBlocksLowerTriangular" | custom-call | tf_op jit(solution)/shard_map/while/body/eval_jaxpr/jit(_cho_solve)/triangular_solve | solution.py:37
  42.2 3.2 %fusion.67 = f32[48,1024]{1,0:T(8,128)S(1)} fusion(f32[]{:T(128)} %get-tuple-element.278, f32[1024]{0:T(1024)S(1)} %bitcast.124, f32[1024]{0:T(1024)S(1)} %bitcast.128, f32[1024]{0:T(1024)S(1)} %bitcast.120, f32[1024]{0:T(1024)S(1)} %bitcast.132, f32[]{:T(128)} %get-tuple-element.275, f32[]{:T(128)} %get-tuple-element.274, ...), kind=kOutput, calls=%fused_computation.9.clone.1.clone | convolution fusion | flops 115392512 | bytes 409612 | tf_op jit(solution)/shard_map/while/body/eval_jaxpr/dot_general | solution.py:32
  45.4 0.4 fusion.70
  45.7 0.3 bitcast_dynamic-update-slice_fusion.7
  46.1 7.4 %multiply_reduce_fusion.7 = f32[]{:T(128)} fusion(f32[48,1024]{1,0:T(8,128)S(1)} %get-tuple-element.222, f32[48,1024]{1,0:T(8,128)S(1)} %get-tuple-element.226, f32[]{:T(128)} %get-tuple-element.278, f32[1024]{0:T(1024)S(1)} %bitcast.125, f32[1024]{0:T(1024)S(1)} %bitcast.129, f32[1024]{0:T(1024)S(1)} %bitcast.121, f32[1024]{0:T(1024)S(1)} %bitcast.133, ...), kind=kOutput, calls=%fused_computation.6.clone.1.clone | convolution fusion | flops 622854144 | bytes 409616 | tf_op jit(solution)/shard_map/while/body/eval_jaxpr/dot_general | solution.py:38
  53.5 0.8 dynamic_update_slice.27
  54.3 4.2 %multiply_reduce_fusion.6 = f32[]{:T(128)} fusion(f32[]{:T(128)} %get-tuple-element.278, f32[1024]{0:T(1024)S(1)} %bitcast.126, f32[1024]{0:T(1024)S(1)} %bitcast.130, f32[1024]{0:T(1024)S(1)} %bitcast.122, f32[1024]{0:T(1024)S(1)} %bitcast.134, f32[]{:T(128)} %get-tuple-element.275, f32[]{:T(128)} %get-tuple-element.274), kind=kLoop, calls=%fused_computation.7.clone.1.clone | loop fusion | flops 15728639 | bytes 16400 | tf_op jit(solution)/shard_map/while/body/eval_jaxpr/reduce_sum | solution.py:78
  58.5 0.8 dynamic_update_slice.26
  59.4 0.7 dynamic_slice.26
  60.0 0.7 iota_compare_fusion.6
  60.7 3.2 %bitcast_dynamic-update-slice_fusion.6 = (f32[2,48,1024]{2,1,0:T(8,128)S(1)}, f32[48,1024]{1,0:T(8,128)S(1)}) fusion(f32[2,48,1024]{2,1,0:T(8,128)S(1)} %get-tuple-element.256, s32[]{:T(128)} %get-tuple-element.255, f32[]{:T(128)} %get-tuple-element.278, f32[1024]{0:T(1024)S(1)} %bitcast.123, f32[1024]{0:T(1024)S(1)} %bitcast.127, ...), kind=kOutput, calls=%fused_computation.12.clone.1.clone | convolution fusion | flops 115392512 | bytes 510976 | tf_op jit(solution)/shard_map/while/body/eval_jaxpr/dot_general | solution.py:29
  63.9 0.9 select_reduce_fusion.7
  64.8 0.1 copy.15
  66.2 0.7 broadcast_select_fusion.3
  66.9 0.1 fusion.68
  66.9 4.4 %cholesky.73 = f32[48,48]{1,0:T(8,128)S(1)} custom-call(f32[48,48]{1,0:T(8,128)S(1)} %fusion.68), custom_call_target="Cholesky" | custom-call | tf_op jit(solution)/shard_map/while/body/eval_jaxpr/jit(cholesky)/cholesky | solution.py:36
  71.3 0.7 compare_reduce_fusion.3
  72.1 0.7 fusion.69
  72.8 3.7 %custom-call.20 = f32[1,48,48]{1,2,0:T(8,128)S(1)} custom-call(f32[1,48,48]{2,1,0:T(8,128)S(1)} %fusion.69), custom_call_target="InvertDiagBlocksLowerTriangular" | custom-call | tf_op jit(solution)/shard_map/while/body/eval_jaxpr/jit(_cho_solve)/triangular_solve | solution.py:37
  76.4 3.2 %fusion.67 = f32[48,1024]{1,0:T(8,128)S(1)} fusion(f32[]{:T(128)} %get-tuple-element.278, f32[1024]{0:T(1024)S(1)} %bitcast.124, f32[1024]{0:T(1024)S(1)} %bitcast.128, f32[1024]{0:T(1024)S(1)} %bitcast.120, f32[1024]{0:T(1024)S(1)} %bitcast.132, f32[]{:T(128)} %get-tuple-element.275, f32[]{:T(128)} %get-tuple-element.274, ...), kind=kOutput, calls=%fused_computation.9.clone.1.clone | convolution fusion | flops 115392512 | bytes 409612 | tf_op jit(solution)/shard_map/while/body/eval_jaxpr/dot_general | solution.py:32
  79.6 0.4 fusion.70
  80.0 0.3 bitcast_dynamic-update-slice_fusion.7
  80.3 7.4 %multiply_reduce_fusion.7 = f32[]{:T(128)} fusion(f32[48,1024]{1,0:T(8,128)S(1)} %get-tuple-element.222, f32[48,1024]{1,0:T(8,128)S(1)} %get-tuple-element.226, f32[]{:T(128)} %get-tuple-element.278, f32[1024]{0:T(1024)S(1)} %bitcast.125, f32[1024]{0:T(1024)S(1)} %bitcast.129, f32[1024]{0:T(1024)S(1)} %bitcast.121, f32[1024]{0:T(1024)S(1)} %bitcast.133, ...), kind=kOutput, calls=%fused_computation.6.clone.1.clone | convolution fusion | flops 622854144 | bytes 409616 | tf_op jit(solution)/shard_map/while/body/eval_jaxpr/dot_general | solution.py:38
  87.8 0.8 dynamic_update_slice.27
  88.6 4.2 %multiply_reduce_fusion.6 = f32[]{:T(128)} fusion(f32[]{:T(128)} %get-tuple-element.278, f32[1024]{0:T(1024)S(1)} %bitcast.126, f32[1024]{0:T(1024)S(1)} %bitcast.130, f32[1024]{0:T(1024)S(1)} %bitcast.122, f32[1024]{0:T(1024)S(1)} %bitcast.134, f32[]{:T(128)} %get-tuple-element.275, f32[]{:T(128)} %get-tuple-element.274), kind=kLoop, calls=%fused_computation.7.clone.1.clone | loop fusion | flops 15728639 | bytes 16400 | tf_op jit(solution)/shard_map/while/body/eval_jaxpr/reduce_sum | solution.py:78
  92.8 0.8 dynamic_update_slice.26
  93.6 0.6 fusion.22
  94.2 39.7 %psum.14 = f32[]{:T(128)} all-reduce(f32[]{:T(128)} %fusion.22), channel_id=1, replica_groups=mesh['prow'=4,'pcol'=8] {'prow','pcol'}, use_global_device_ids=true, to_apply=%region_8.9 | all-reduce | flops 1 | bytes 8 | tf_op jit(solution)/shard_map/psum | solution.py:89
  134.6 0.5 fusion.25
  135.1 1.0 select_bitcast_fusion
  136.2 0.6 select_reduce_fusion.2
  136.8 41.0 %psum.15 = s32[1]{0:T(128)} all-reduce(s32[1]{0:T(128)} %bitcast.25), channel_id=1, replica_groups=mesh['prow'=4,'pcol'=8] {'prow','pcol'}, use_global_device_ids=true, to_apply=%region_10.11 | all-reduce | flops 1 | bytes 8 | tf_op jit(solution)/shard_map/psum | solution.py:68
  (19 shorter events, 0.2 us)
Async XLA Ops:
  0.6 23.7 %copy-start.1 = (s32[2,1,1,1]{0,3,2,1:T(1,128)S(1)}, s32[2,1,1,1]{0,3,2,1:T(1,128)}, u32[]{:S(2)}) copy-start(s32[2,1,1,1]{0,3,2,1:T(1,128)} %param.12) | copy-start | bytes 28
  24.4 0.7 copy-start
where the time goes:
time: 178 us
  blocking collectives  102 us (57%)
  other arithmetic  33.2 us (19%)
  matrix products  30.7 us (17%)
  local copies, waits for them, and re-layouts  6.5 us (4%)
  between operations  2.82 us (2%)
  loops' own time  2.75 us (2%)
    psum x1, blocking collectives, per_device(): rank_sum = lax.psum(ranks_local, ('prow', 'pcol'))  41 us
    psum x1, blocking collectives, per_device(): total = lax.psum(norm_local, ('prow', 'pcol'))  39.7 us
    dot_general x2, matrix products, compress(): lax.dot_general(sketched, coeffs, (((0,), (0,)), ((), ())), precision=lax...  14.9 us
    all_gather x1, blocking collectives, per_device(): gathered = lax.all_gather(points, 'pcol', axis=1, tiled=True)  10.9 us
    another operation x6, other arithmetic, compress(): factor = jnp.linalg.cholesky(gram)  10.3 us
    all_gather x1, blocking collectives, per_device(): bank_whole = lax.all_gather(sketch_bank, 'pcol', axis=0, tiled=True)  10.2 us
    another operation x4, other arithmetic, compress(): coeffs = jax.scipy.linalg.cho_solve((factor, True), product)  8.74 us
    reduce_sum x2, other arithmetic, one_tile(): norm_sq = jnp.sum(tile_block * tile_block)  8.47 us

commit v1 on v0

--- a/solution.py
+++ b/solution.py
@@ -66,7 +66,19 @@
     offdiag = slot_col < slot_row
     ranks_local = jnp.sum(jnp.where(offdiag, own_ranks, 0))
     rank_sum = lax.psum(ranks_local, ("prow", "pcol"))
-    bank_whole = lax.all_gather(sketch_bank, "pcol", axis=0, tiled=True)
+    ndev = jax.lax.axis_size("pcol")
+    leaves = [sketch_bank]
+    for ix in range(ndev - 1):
+        leaves.append(
+            jax.lax.ppermute(
+                leaves[-1], axis_name="pcol", perm=[(j0, (j0 + 1) % ndev) for j0 in range(ndev)]
+            )
+        )
+    bank_whole = jnp.roll(
+        jnp.concatenate(leaves[::-1], axis=0),
+        shift=(jax.lax.axis_index("pcol") + 1) * sketch_bank.shape[0],
+        axis=0,
+    )
     chosen = bank_whole[own_ids]
     row_points_all = every_block[slot_row]
     col_points_all = every_block[slot_col]

time: 178 us -> 194 us (1.090)
  waiting for transfers between devices: 0 us -> 25.7 us
  blocking collectives: 102 us -> 91.1 us
    ppermute x0 -> x7, waiting for transfers between devices: none -> 25.7 us  [per_device(): jax.lax.ppermute(leaves[-1], axis_name='pcol', perm=[(j0, (j0 + 1) % ndev...]
    all_gather x1 -> x0, blocking collectives: 10.2 us -> none  [per_device(): bank_whole = lax.all_gather(sketch_bank, 'pcol', axis=0, tiled=True)]
  transfers between devices with their start and end apart: 0 -> 7, of which waited for: 0 -> 6; matrix products, arithmetic and copies ran while one was open for 0% -> 2% of each run, Pallas kernels for 0% -> 0%
where the time goes in v1:
time: 194 us; the launch traced here: 193 us
  blocking collectives  91.1 us (47%)
  other arithmetic  33.5 us (17%)
  matrix products  30.5 us (16%)
  waiting for transfers between devices  25.7 us (13%)
  local copies, waits for them, and re-layouts  6.03 us (3%)
  between operations  2.93 us (2%)
  loops' own time  2.64 us (1%)
    psum x1, blocking collectives, per_device(): total = lax.psum(norm_local, ('prow', 'pcol'))  41.3 us
    psum x1, blocking collectives, per_device(): rank_sum = lax.psum(ranks_local, ('prow', 'pcol'))  39.8 us
    ppermute x7, waiting for transfers between devices, per_device(): jax.lax.ppermute(leaves[-1], axis_name='pcol', perm=[(j0, (j0 + 1) % ndev...  25.7 us
    dot_general x2, matrix products, compress(): lax.dot_general(sketched, coeffs, (((0,), (0,)), ((), ())), precision=lax...  14.7 us
    another operation x6, other arithmetic, compress(): factor = jnp.linalg.cholesky(gram)  10.1 us
    all_gather x1, blocking collectives, per_device(): gathered = lax.all_gather(points, 'pcol', axis=1, tiled=True)  9.98 us
    another operation x4, other arithmetic, compress(): coeffs = jax.scipy.linalg.cho_solve((factor, True), product)  8.47 us
    reduce_sum x2, other arithmetic, one_tile(): norm_sq = jnp.sum(tile_block * tile_block)  8.3 us
  transfers between devices with their start and end apart: 7, of which 6 were waited for; matrix products, arithmetic and copies ran while one was open for 2% of the time, Pallas kernels for 0%

profile of v1, /device:TPU:0, one launch (start us, length us, event | category | flops | bytes accessed | tf_op | source)
XLA Modules:
  0.0 193.4 jit_solution(9845030584155538405)
XLA Ops:
  0.6 0.5 collective-permute-start
  1.2 5.4 %collective-permute-done = bf16[1,48,1024]{2,1,0:T(8,128)(2,1)S(1)} collective-permute-done((bf16[1,48,1024]{2,1,0:T(8,128)(2,1)}, bf16[1,48,1024]{2,1,0:T(8,128)(2,1)S(1)}, u32[]{:S(2)}, u32[]{:S(2)}) %collective-permute-start) | collective-permute-done | bytes 98336 | tf_op jit(solution)/shard_map/ppermute | solution.py:73
  6.6 0.7 fusion.23
  7.2 10.0 %all_gather.3 = f32[1,8,2,1024]{3,2,0,1:T(2,128)S(1)} all-gather(f32[1,1,2,1024]{3,2,0,1:T(2,128)} %bitcast.135), channel_id=1, replica_groups=mesh['prow'=4,'pcol'=8] {'pcol'}, dimensions={1}, use_global_device_ids=true | all-gather | bytes 73728 | tf_op jit(solution)/shard_map/all_gather | solution.py:57
  17.2 0.4 collective-permute-start.2
  17.6 0.6 gather_fusion.2
  18.2 4.0 %collective-permute-done.2 = bf16[1,48,1024]{2,1,0:T(8,128)(2,1)S(1)} collective-permute-done((bf16[1,48,1024]{2,1,0:T(8,128)(2,1)S(1)}, bf16[1,48,1024]{2,1,0:T(8,128)(2,1)S(1)}, u32[]{:S(2)}, u32[]{:S(2)}) %collective-permute-start.2) | collective-permute-done | bytes 98336 | tf_op jit(solution)/shard_map/ppermute | solution.py:73
  22.2 4.9 %collective-permute-done.3 = bf16[1,48,1024]{2,1,0:T(8,128)(2,1)S(1)} collective-permute-done((bf16[1,48,1024]{2,1,0:T(8,128)(2,1)S(1)}, bf16[1,48,1024]{2,1,0:T(8,128)(2,1)S(1)}, u32[]{:S(2)}, u32[]{:S(2)}) %collective-permute-start.3) | collective-permute-done | bytes 98336 | tf_op jit(solution)/shard_map/ppermute | solution.py:73
  27.1 0.6 gather_fusion.1
  29.1 3.0 %collective-permute-done.4 = bf16[1,48,1024]{2,1,0:T(8,128)(2,1)S(1)} collective-permute-done((bf16[1,48,1024]{2,1,0:T(8,128)(2,1)S(1)}, bf16[1,48,1024]{2,1,0:T(8,128)(2,1)S(1)}, u32[]{:S(2)}, u32[]{:S(2)}) %collective-permute-start.4) | collective-permute-done | bytes 98336 | tf_op jit(solution)/shard_map/ppermute | solution.py:73
  32.1 1.4 select_reduce_fusion.2
  33.4 3.6 %collective-permute-done.5 = bf16[1,48,1024]{2,1,0:T(8,128)(2,1)S(1)} collective-permute-done((bf16[1,48,1024]{2,1,0:T(8,128)(2,1)S(1)}, bf16[1,48,1024]{2,1,0:T(8,128)(2,1)S(1)}, u32[]{:S(2)}, u32[]{:S(2)}) %collective-permute-start.5) | collective-permute-done | bytes 98336 | tf_op jit(solution)/shard_map/ppermute | solution.py:73
  37.0 4.9 %collective-permute-done.6 = bf16[1,48,1024]{2,1,0:T(8,128)(2,1)S(1)} collective-permute-done((bf16[1,48,1024]{2,1,0:T(8,128)(2,1)S(1)}, bf16[1,48,1024]{2,1,0:T(8,128)(2,1)S(1)}, u32[]{:S(2)}, u32[]{:S(2)}) %collective-permute-start.6) | collective-permute-done | bytes 98336 | tf_op jit(solution)/shard_map/ppermute | solution.py:73
  42.3 0.6 gather_fusion
  43.0 66.5 %while.17 = (s32[]{:T(128)}, f32[2,48,1024]{2,1,0:T(8,128)S(1)}, f32[2,48,1024]{2,1,0:T(8,128)S(1)}, f32[2]{0:T(128)S(1)}, f32[2]{0:T(128)S(1)}, /*index=5*/s32[...) while((s32[]{:T(128)}, f32[2,48,1024]{2,1,0:T(8,128)S(1)}, ...), condition=%wide.region_6.7_spmd.clone, body=%wide.region_0.6_spmd.sunk.clone | while | flops 954344128 | bytes 2676799 | solution.py:97
  43.0 0.6 dynamic_slice.32
  43.6 0.6 iota_compare_fusion.6
  44.2 3.2 %bitcast_dynamic-update-slice_fusion.6 = (f32[2,48,1024]{2,1,0:T(8,128)S(1)}, f32[48,1024]{1,0:T(8,128)S(1)}) fusion(f32[2,48,1024]{2,1,0:T(8,128)S(1)} %get-tuple-element.258, s32[]{:T(128)} %get-tuple-element.257, f32[]{:T(128)} %get-tuple-element.280, f32[1024]{0:T(1024)S(1)} %bitcast.123, f32[1024]{0:T(1024)S(1)} %bitcast.127, ...), kind=kOutput, calls=%fused_computation.12.clone.1.clone | convolution fusion | flops 115392512 | bytes 510976 | tf_op jit(solution)/shard_map/while/body/eval_jaxpr/dot_general | solution.py:29
  47.3 0.9 select_reduce_fusion.7
  49.6 0.6 broadcast_select_fusion.3
  50.2 4.4 %cholesky.73 = f32[48,48]{1,0:T(8,128)S(1)} custom-call(f32[48,48]{1,0:T(8,128)S(1)} %fusion.68), custom_call_target="Cholesky" | custom-call | tf_op jit(solution)/shard_map/while/body/eval_jaxpr/jit(cholesky)/cholesky | solution.py:36
  54.6 0.6 compare_reduce_fusion.3
  55.3 0.6 fusion.69
  55.8 3.7 %custom-call.22 = f32[1,48,48]{1,2,0:T(8,128)S(1)} custom-call(f32[1,48,48]{2,1,0:T(8,128)S(1)} %fusion.69), custom_call_target="InvertDiagBlocksLowerTriangular" | custom-call | tf_op jit(solution)/shard_map/while/body/eval_jaxpr/jit(_cho_solve)/triangular_solve | solution.py:37
  59.5 3.2 %fusion.67 = f32[48,1024]{1,0:T(8,128)S(1)} fusion(f32[]{:T(128)} %get-tuple-element.280, f32[1024]{0:T(1024)S(1)} %bitcast.124, f32[1024]{0:T(1024)S(1)} %bitcast.128, f32[1024]{0:T(1024)S(1)} %bitcast.120, f32[1024]{0:T(1024)S(1)} %bitcast.132, f32[]{:T(128)} %get-tuple-element.277, f32[]{:T(128)} %get-tuple-element.276, ...), kind=kOutput, calls=%fused_computation.9.clone.1.clone | convolution fusion | flops 115392512 | bytes 409612 | tf_op jit(solution)/shard_map/while/body/eval_jaxpr/dot_general | solution.py:32
  63.4 7.3 %multiply_reduce_fusion.7 = f32[]{:T(128)} fusion(f32[48,1024]{1,0:T(8,128)S(1)} %get-tuple-element.224, f32[48,1024]{1,0:T(8,128)S(1)} %get-tuple-element.228, f32[]{:T(128)} %get-tuple-element.280, f32[1024]{0:T(1024)S(1)} %bitcast.125, f32[1024]{0:T(1024)S(1)} %bitcast.129, f32[1024]{0:T(1024)S(1)} %bitcast.121, f32[1024]{0:T(1024)S(1)} %bitcast.133, ...), kind=kOutput, calls=%fused_computation.6.clone.1.clone | convolution fusion | flops 622854144 | bytes 409616 | tf_op jit(solution)/shard_map/while/body/eval_jaxpr/dot_general | solution.py:38
  70.7 0.7 dynamic_update_slice.27
  71.4 4.1 %multiply_reduce_fusion.6 = f32[]{:T(128)} fusion(f32[]{:T(128)} %get-tuple-element.280, f32[1024]{0:T(1024)S(1)} %bitcast.126, f32[1024]{0:T(1024)S(1)} %bitcast.130, f32[1024]{0:T(1024)S(1)} %bitcast.122, f32[1024]{0:T(1024)S(1)} %bitcast.134, f32[]{:T(128)} %get-tuple-element.277, f32[]{:T(128)} %get-tuple-element.276), kind=kLoop, calls=%fused_computation.7.clone.1.clone | loop fusion | flops 15728639 | bytes 16400 | tf_op jit(solution)/shard_map/while/body/eval_jaxpr/reduce_sum | solution.py:90
  75.5 0.7 dynamic_update_slice.26
  76.2 0.6 dynamic_slice.32
  76.8 0.6 iota_compare_fusion.6
  77.4 3.2 %bitcast_dynamic-update-slice_fusion.6 = (f32[2,48,1024]{2,1,0:T(8,128)S(1)}, f32[48,1024]{1,0:T(8,128)S(1)}) fusion(f32[2,48,1024]{2,1,0:T(8,128)S(1)} %get-tuple-element.258, s32[]{:T(128)} %get-tuple-element.257, f32[]{:T(128)} %get-tuple-element.280, f32[1024]{0:T(1024)S(1)} %bitcast.123, f32[1024]{0:T(1024)S(1)} %bitcast.127, ...), kind=kOutput, calls=%fused_computation.12.clone.1.clone | convolution fusion | flops 115392512 | bytes 510976 | tf_op jit(solution)/shard_map/while/body/eval_jaxpr/dot_general | solution.py:29
  80.5 0.9 select_reduce_fusion.7
  82.8 0.6 broadcast_select_fusion.3
  83.4 4.4 %cholesky.73 = f32[48,48]{1,0:T(8,128)S(1)} custom-call(f32[48,48]{1,0:T(8,128)S(1)} %fusion.68), custom_call_target="Cholesky" | custom-call | tf_op jit(solution)/shard_map/while/body/eval_jaxpr/jit(cholesky)/cholesky | solution.py:36
  87.9 0.6 compare_reduce_fusion.3
  88.5 0.6 fusion.69
  89.1 3.7 %custom-call.22 = f32[1,48,48]{1,2,0:T(8,128)S(1)} custom-call(f32[1,48,48]{2,1,0:T(8,128)S(1)} %fusion.69), custom_call_target="InvertDiagBlocksLowerTriangular" | custom-call | tf_op jit(solution)/shard_map/while/body/eval_jaxpr/jit(_cho_solve)/triangular_solve | solution.py:37
  92.7 3.2 %fusion.67 = f32[48,1024]{1,0:T(8,128)S(1)} fusion(f32[]{:T(128)} %get-tuple-element.280, f32[1024]{0:T(1024)S(1)} %bitcast.124, f32[1024]{0:T(1024)S(1)} %bitcast.128, f32[1024]{0:T(1024)S(1)} %bitcast.120, f32[1024]{0:T(1024)S(1)} %bitcast.132, f32[]{:T(128)} %get-tuple-element.277, f32[]{:T(128)} %get-tuple-element.276, ...), kind=kOutput, calls=%fused_computation.9.clone.1.clone | convolution fusion | flops 115392512 | bytes 409612 | tf_op jit(solution)/shard_map/while/body/eval_jaxpr/dot_general | solution.py:32
  96.6 7.3 %multiply_reduce_fusion.7 = f32[]{:T(128)} fusion(f32[48,1024]{1,0:T(8,128)S(1)} %get-tuple-element.224, f32[48,1024]{1,0:T(8,128)S(1)} %get-tuple-element.228, f32[]{:T(128)} %get-tuple-element.280, f32[1024]{0:T(1024)S(1)} %bitcast.125, f32[1024]{0:T(1024)S(1)} %bitcast.129, f32[1024]{0:T(1024)S(1)} %bitcast.121, f32[1024]{0:T(1024)S(1)} %bitcast.133, ...), kind=kOutput, calls=%fused_computation.6.clone.1.clone | convolution fusion | flops 622854144 | bytes 409616 | tf_op jit(solution)/shard_map/while/body/eval_jaxpr/dot_general | solution.py:38
  104.0 0.7 dynamic_update_slice.27
  104.6 4.1 %multiply_reduce_fusion.6 = f32[]{:T(128)} fusion(f32[]{:T(128)} %get-tuple-element.280, f32[1024]{0:T(1024)S(1)} %bitcast.126, f32[1024]{0:T(1024)S(1)} %bitcast.130, f32[1024]{0:T(1024)S(1)} %bitcast.122, f32[1024]{0:T(1024)S(1)} %bitcast.134, f32[]{:T(128)} %get-tuple-element.277, f32[]{:T(128)} %get-tuple-element.276), kind=kLoop, calls=%fused_computation.7.clone.1.clone | loop fusion | flops 15728639 | bytes 16400 | tf_op jit(solution)/shard_map/while/body/eval_jaxpr/reduce_sum | solution.py:90
  108.8 0.7 dynamic_update_slice.26
  109.4 0.6 fusion.22
  110.0 39.8 %psum.15 = s32[1]{0:T(128)} all-reduce(s32[1]{0:T(128)} %bitcast.25), channel_id=1, replica_groups=mesh['prow'=4,'pcol'=8] {'prow','pcol'}, use_global_device_ids=true, to_apply=%region_10.11 | all-reduce | flops 1 | bytes 8 | tf_op jit(solution)/shard_map/psum | solution.py:68
  149.8 41.3 %psum.14 = f32[]{:T(128)} all-reduce(f32[]{:T(128)} %fusion.22), channel_id=1, replica_groups=mesh['prow'=4,'pcol'=8] {'prow','pcol'}, use_global_device_ids=true, to_apply=%region_8.9 | all-reduce | flops 1 | bytes 8 | tf_op jit(solution)/shard_map/psum | solution.py:101
  191.9 0.5 fusion.25
  192.4 1.0 select_bitcast_fusion
  (48 shorter events, 2.1 us)
Async XLA Ops:
  0.6 41.4 %copy-start = (bf16[1,48,1024]{2,1,0:T(8,128)(2,1)S(1)}, bf16[1,48,1024]{2,1,0:T(8,128)(2,1)}, u32[]{:S(2)}) copy-start(bf16[1,48,1024]{2,1,0:T(8,128)(2,1)} %param.11) | copy-start | bytes 294916
  0.6 5.9 %collective-permute-start = (bf16[1,48,1024]{2,1,0:T(8,128)(2,1)}, bf16[1,48,1024]{2,1,0:T(8,128)(2,1)S(1)}, u32[]{:S(2)}, u32[]{:S(2)}) collective-permute-start(bf16[1,48,1024]{2,1,0:T(8,128)(2,1)} %param.11), channel_id=1, source_target_pairs={{0,1},{1,2},{2,3},{3,4},{4,5},{5,6},{6,7},{7,0},{8,9},{9,10},{10,1... | collective-permute-start | bytes 294920 | tf_op jit(solution)/shard_map/ppermute | solution.py:73
  6.6 10.7 %collective-permute-start.1 = (bf16[1,48,1024]{2,1,0:T(8,128)(2,1)S(1)}, bf16[1,48,1024]{2,1,0:T(8,128)(2,1)S(1)}, u32[]{:S(2)}, u32[]{:S(2)}) collective-permute-start(bf16[1,48,1024]{2,1,0:T(8,128)(2,1)S(1)} %collective-permute-done), channel_id=1, source_target_pairs={{0,1},{1,2},{2,3},{3,4},{4,5},{5,6},{6,7},{7,0},{8,9},{9,10},{10,1... | collective-permute-start | bytes 294920 | tf_op jit(solution)/shard_map/ppermute | solution.py:73
  17.2 4.9 %collective-permute-start.2 = (bf16[1,48,1024]{2,1,0:T(8,128)(2,1)S(1)}, bf16[1,48,1024]{2,1,0:T(8,128)(2,1)S(1)}, u32[]{:S(2)}, u32[]{:S(2)}) collective-permute-start(bf16[1,48,1024]{2,1,0:T(8,128)(2,1)S(1)} %collective-permute-done.1), channel_id=1, source_target_pairs={{0,1},{1,2},{2,3},{3,4},{4,5},{5,6},{6,7},{7,0},{8,9},{9,10},{10,1... | collective-permute-start | bytes 294920 | tf_op jit(solution)/shard_map/ppermute | solution.py:73
  22.2 4.9 %collective-permute-start.3 = (bf16[1,48,1024]{2,1,0:T(8,128)(2,1)S(1)}, bf16[1,48,1024]{2,1,0:T(8,128)(2,1)S(1)}, u32[]{:S(2)}, u32[]{:S(2)}) collective-permute-start(bf16[1,48,1024]{2,1,0:T(8,128)(2,1)S(1)} %collective-permute-done.2), channel_id=1, source_target_pairs={{0,1},{1,2},{2,3},{3,4},{4,5},{5,6},{6,7},{7,0},{8,9},{9,10},{10,1... | collective-permute-start | bytes 294920 | tf_op jit(solution)/shard_map/ppermute | solution.py:73
  27.1 4.9 %collective-permute-start.4 = (bf16[1,48,1024]{2,1,0:T(8,128)(2,1)S(1)}, bf16[1,48,1024]{2,1,0:T(8,128)(2,1)S(1)}, u32[]{:S(2)}, u32[]{:S(2)}) collective-permute-start(bf16[1,48,1024]{2,1,0:T(8,128)(2,1)S(1)} %collective-permute-done.3), channel_id=1, source_target_pairs={{0,1},{1,2},{2,3},{3,4},{4,5},{5,6},{6,7},{7,0},{8,9},{9,10},{10,1... | collective-permute-start | bytes 294920 | tf_op jit(solution)/shard_map/ppermute | solution.py:73
  32.1 4.9 %collective-permute-start.5 = (bf16[1,48,1024]{2,1,0:T(8,128)(2,1)S(1)}, bf16[1,48,1024]{2,1,0:T(8,128)(2,1)S(1)}, u32[]{:S(2)}, u32[]{:S(2)}) collective-permute-start(bf16[1,48,1024]{2,1,0:T(8,128)(2,1)S(1)} %collective-permute-done.4), channel_id=1, source_target_pairs={{0,1},{1,2},{2,3},{3,4},{4,5},{5,6},{6,7},{7,0},{8,9},{9,10},{10,1... | collective-permute-start | bytes 294920 | tf_op jit(solution)/shard_map/ppermute | solution.py:73
  37.0 4.9 %collective-permute-start.6 = (bf16[1,48,1024]{2,1,0:T(8,128)(2,1)S(1)}, bf16[1,48,1024]{2,1,0:T(8,128)(2,1)S(1)}, u32[]{:S(2)}, u32[]{:S(2)}) collective-permute-start(bf16[1,48,1024]{2,1,0:T(8,128)(2,1)S(1)} %collective-permute-done.5), channel_id=1, source_target_pairs={{0,1},{1,2},{2,3},{3,4},{4,5},{5,6},{6,7},{7,0},{8,9},{9,10},{10,1... | collective-permute-start | bytes 294920 | tf_op jit(solution)/shard_map/ppermute | solution.py:73
  42.2 0.8 copy-start.1
